TPU v7x, 32 devices: a whole 2x2x4 slice. The times are simulated.
32 devices in a mesh: face: 4 (over z), tile: 4 (over y, core), lev: 2 (over x).
Axes of the slice: x: 2, y: 2, z: 4, core: 2. Of those that a mesh axis runs over, the one named last changes fastest.
Arguments:
- airflow_components: float32 [2, 36, 32, 512], P(None, 'lev', 'face', 'tile'), may hold values from -4.5 to 4.5, as said below
- heat_state: float32 [36, 32, 512], P('lev', 'face', 'tile'), may hold values from 0.5 to 2
- layer_pressure_depth: float32 [36, 32, 512], P('lev', 'face', 'tile'), may hold values from 0.5 to 2
- constituent_masses: float32 [18, 36, 32, 512], P(None, 'lev', 'face', 'tile'), may hold values from 0.1 to 1
- ground_gravity_potential: float32 [32, 512], P('face', 'tile'), may hold values from -8 to 8
- inverse_mapping_entries: float32 [4, 32, 512], P(None, 'face', 'tile'), may hold values from -4 to 4
- mapping_determinant: float32 [32, 512], P('face', 'tile'), may hold values from 0.5 to 2
- interface_rightangle_rotations: int32 [4, 4, 2], replicated, may hold values from 0 to 3
- interface_flipped_markers: int32 [4, 4, 2], replicated, may hold values from 0 to 1
- corner_block_tally: int32 [4, 4], replicated, may hold values from 3 to 4
Outputs:
- airflow_next: float32 [2, 36, 32, 512], P(None, 'lev', 'face', 'tile')
- heat_state_next: float32 [36, 32, 512], P('lev', 'face', 'tile')
- pressure_depth_next: float32 [36, 32, 512], P('lev', 'face', 'tile')
- constituent_masses_next: float32 [18, 36, 32, 512], P(None, 'lev', 'face', 'tile')
- stepping_bounds: float32 [2], replicated
Inputs may be any that keep to these rules, and one draw needn't show every extreme that they name: `airflow_components`: component magnitudes grow across the grid by up to a factor of 9. `interface_rightangle_rotations`: entry [f, t, 0] concerns the boundary between blocks (f, t) and (f+1, t), entry [f, t, 1] the one between (f, t) and (f, t+1). `interface_flipped_markers`: indexed like interface_rightangle_rotations. `corner_block_tally`: entry [f, t] belongs to the corner shared by blocks (f, t), (f+1, t), (f, t+1), (f+1, t+1).
All inputs are finite; a program needn't handle non-finite values.
Results may differ from a plain program's by a relative error of at most 0.00012.
Values sent between devices are 32-bit elements; how exact they have to be, the bound alone decides.
A program may use at most 64 MiB of HBM per device.

v0:
```python
import functools
import math

import jax
import jax.numpy as jnp
import numpy as np
from jax import lax
from jax.experimental import pallas as pl
from jax.experimental.pallas import tpu as pltpu
from jax.sharding import PartitionSpec as P

time_step = 0.05
viscosity = 0.05
f32 = jnp.float32
bf16 = jnp.bfloat16
MESH = pl.DeviceIdType.MESH
highest = lax.Precision.HIGHEST


def gll_tables():
    offset = 1.0 / math.sqrt(5.0)
    nodes = np.array([-1.0, -offset, offset, 1.0])
    weights = np.array([1.0 / 6.0, 5.0 / 6.0, 5.0 / 6.0, 1.0 / 6.0])
    bary = np.ones(4)
    for i in range(4):
        for j in range(4):
            if j != i:
                bary[i] = bary[i] / (nodes[i] - nodes[j])
    derivative = np.zeros((4, 4))
    for i in range(4):
        for j in range(4):
            if j != i:
                derivative[i, j] = bary[j] / bary[i] / (nodes[i] - nodes[j])
        derivative[i, i] = -np.sum(derivative[i])
    return derivative, weights


def lane_tables(columns):
    derivative, weights = gll_tables()
    d = np.kron(np.eye(columns // 4), derivative)
    s = np.eye(columns)
    for c in range(columns - 1):
        if c % 4 == 3:
            s[c, c + 1] = s[c + 1, c] = 1.0
    w = np.tile(weights, columns // 4)
    t = (-time_step * (d.T * w[None, :]) @ s).astype(np.float32)
    t_hi = jnp.asarray(t).astype(bf16)
    t_lo = (jnp.asarray(t) - t_hi.astype(f32)).astype(bf16)
    sb = jnp.asarray(s, bf16)
    d_t = jnp.asarray(d.T, f32)
    d_hi = d_t.astype(bf16)
    d_lo = (d_t - d_hi.astype(f32)).astype(bf16)
    return jnp.concatenate([sb, sb, t_hi, t_hi, t_lo], 0), jnp.concatenate([d_hi, d_hi, d_lo], 0), jnp.asarray(w[None, :], f32)


def split(x):
    hi = x.astype(bf16)
    return hi, (x - hi.astype(f32)).astype(bf16)


def layout(levels, tracers):
    group = 8 // math.gcd(levels, 8)
    chunks, q = [], 0
    while q < tracers:
        n = min(group, tracers - q)
        chunks.append((q * levels, -(-n * levels // 8) * 8, n * levels))
        q += n
    return chunks


def packing(levels, chunks):
    out = [(0, 1, 1)]
    for tiles in [c[1] // 8 for c in chunks] + [2 * (levels // 8) + 1] * 2:
        quads = (tiles - 1) // 4
        out.append((quads, tiles - quads, 8 * (tiles - quads)))
    return out


def kernel(
    sizes, dims,
    wind_h, temp_h, thick_h, tracer_h, ground_h, maps_h, det_h, ops_h, dct_h, wc_h,
    rot_h, flip_h, tally_h,
    wind_o, temp_o, thick_o, tracer_o, bound_o,
    wind, temp, thick, tracer, geo, ground, maps, det, ops, dct, wc,
    a_ref, b_ref, z_ref, below, above_ref, pack, corner, total, peak,
    up_in, down_in, left_in, right_in, corner_in, total_in, peak_in,
    rot_ref, flip_ref, tally_ref,
    in_sem, sent_sem, piece_sem, corner_sem, total_sem, peak_sem,
):
    nf, nt, nl = sizes
    levels, rows, columns, chunks, pad = dims
    derivative, weights = gll_tables()
    rep = [a - (a // 4) for a in range(rows)]
    distinct = rows - rows // 4 + 1
    face, tile, lev = lax.axis_index("face"), lax.axis_index("tile"), lax.axis_index("lev")
    f_up, f_dn = lax.rem(face + nf - 1, nf), lax.rem(face + 1, nf)
    t_lf, t_rt = lax.rem(tile + nt - 1, nt), lax.rem(tile + 1, nt)

    pieces = [(0, 8, 1)]
    at = 8
    for _, count, _ in chunks:
        pieces.append((at, count, 1))
        at += count
    pieces.append((at, 2 * pad, 1))
    pieces.append((at + 2 * pad, 2 * pad, 2))
    first_pack = np.cumsum([0] + [p[2] for p in pieces]).tolist()
    last = len(pieces) - 1
    heat = last - 1
    full, tail = levels // 8, levels % 8
    packed = packing(levels, chunks)
    first_row = np.cumsum([0] + [8 * p[1] for p in packed]).tolist()
    quarter = columns // 4
    side_rows = [1] + [8 * p[2] for p in pieces[1:]]

    n = levels * rows
    groups_in = [
        [(maps_h, maps), (det_h, det), (wc_h, wc),
         (wind_h.at[0], wind.at[0, :n]), (wind_h.at[1], wind.at[1, :n])],
        [(temp_h, temp.at[:n]), (thick_h, thick.at[:n])],
        [(ops_h, ops)],
        [(dct_h, dct), (ground_h, ground)],
    ]
    group_rows = [5 * rows + 1 + 2 * n, 2 * n, 5 * columns // 2, 3 * columns // 2 + rows]
    n0 = len(groups_in)
    spans = [pl.ds(start * rows, valid * rows) for start, _, valid in chunks]
    traced = [
        pltpu.make_async_copy(tracer_h.at[span], tracer.at[span], in_sem.at[n0 + k])
        for k, span in enumerate(spans)
    ]
    tables = [(rot_h, rot_ref), (flip_h, flip_ref), (tally_h, tally_ref)]
    at = n0 + len(chunks)
    tables = [pltpu.make_async_copy(s, d, in_sem.at[at + i]) for i, (s, d) in enumerate(tables)]

    def fetch(i):
        for s, d in groups_in[i]:
            pltpu.make_async_copy(s, d, in_sem.at[i]).start()

    def drain(count, sem):
        view = z_ref.at[0, pl.ds(0, count)] if count <= z_ref.shape[1] else tracer.at[pl.ds(0, count)]
        pltpu.make_async_copy(view, view, sem).wait()

    fetch(0)
    traced[0].start()
    fetch(2)
    fetch(1)
    for load in traced[1:]:
        load.start()
    fetch(3)
    for load in tables:
        load.start()

    peers = [(lax.rem(face + o, nf), tile, lev) for o in range(1, nf)]
    peers += [(face, lax.rem(tile + o, nt), lev) for o in range(1, nt)]
    peers += [(face, tile, lax.rem(lev + o, nl)) for o in range(1, nl)]
    diagonals = [(f_dn, t_rt, lev), (f_dn, t_lf, lev), (f_up, t_rt, lev), (f_up, t_lf, lev)]
    barrier = pltpu.get_barrier_semaphore()
    for peer in peers + diagonals:
        pl.semaphore_signal(barrier, inc=1, device_id=peer, device_id_type=MESH)

    extra = (pad - levels) * rows
    if extra:
        zero = jnp.zeros((extra, columns), f32)
        temp[levels * rows :, :] = zero
        thick[levels * rows :, :] = zero
        geo[levels * rows :, :] = zero
        wind[0, levels * rows :, :] = zero
        wind[1, levels * rows :, :] = zero
    end = chunks[-1][0] + chunks[-1][2]
    more = chunks[-1][1] - chunks[-1][2]
    if more:
        tracer[end * rows :, :] = jnp.zeros((more * rows, columns), f32)

    sent = []

    def send(src, dst, r, to):
        pltpu.make_async_remote_copy(
            src_ref=src, dst_ref=dst, send_sem=sent_sem.at[0], recv_sem=r,
            device_id=to, device_id_type=MESH,
        ).start()
        sent.append(math.prod(src.shape) // columns)

    def column_sums():
        drain(group_rows[1], in_sem.at[1])
        acc = jnp.zeros((rows, columns), f32)
        for k in reversed(range(levels)):
            term = temp[k * rows : (k + 1) * rows, :] * thick[k * rows : (k + 1) * rows, :]
            geo[k * rows : (k + 1) * rows, :] = acc + 0.5 * term
            acc = acc + term
        total[...] = acc
        for o in range(1, nl):
            send(total, total_in.at[o - 1], total_sem.at[0], (face, tile, lax.rem(lev + o, nl)))

    drain(group_rows[0], in_sem.at[0])
    w_col = wc[...]
    drain(group_rows[2], in_sem.at[2])
    table = ops[...]
    narrow = ops[: 2 * columns, :]
    wr = [float(weights[a % 4]) for a in range(rows)]
    m = [[maps[e * rows + a : e * rows + a + 1, :] for a in range(rows)] for e in range(4)]
    jac = [det[a : a + 1, :] for a in range(rows)]
    mass = [jac[a] * (wr[a] * w_col) for a in range(rows)]
    step_d = [[float(time_step * wr[a] * derivative[a % 4, b]) for b in range(4)] for a in range(rows)]
    dd = [[float(derivative[i, j]) for j in range(4)] for i in range(4)]

    def level_rows(ref, a):
        return ref[pl.ds(a, pad, stride=rows), :]

    def along_rows(values, a, coef):
        base = a - a % 4
        out = coef[0] * values[base]
        for b in range(1, 4):
            out = out + coef[b] * values[base + b]
        return out

    def merged(values):
        out = [None] * distinct
        for a in range(rows):
            r = rep[a]
            out[r] = values[a] if out[r] is None else out[r] + values[a]
        return out

    def lanes_plain(x):
        hi, lo = split(x)
        return jnp.dot(jnp.concatenate([hi, lo], 1), narrow, preferred_element_type=f32)

    def lanes_both(p, g):
        ph, plo = split(p)
        gh, glo = split(g)
        return jnp.dot(
            jnp.concatenate([ph, plo, gh, glo, gh], 1), table, preferred_element_type=f32
        )

    def by_column(values):
        stacked = jnp.concatenate(values, 0)
        hi, lo = split(stacked)
        out = jnp.dot(
            jnp.concatenate([hi, lo, hi], 1), dct[...], preferred_element_type=f32
        )
        n = values[0].shape[0]
        return [out[i * n : (i + 1) * n] for i in range(len(values))]

    lane = lax.broadcasted_iota(jnp.int32, (8, columns), 1)
    unit = 2 * distinct
    within = lax.rem(lane, unit)

    def put(piece, offset, r, z):
        z_ref[r, piece + offset : piece + offset + z.shape[0], :] = z

    def pack_of(start, groups):
        out = jnp.zeros((8, columns), f32)
        for i in range(groups):
            for r in range(distinct):
                spot = unit * i + 2 * r
                value = pltpu.roll(z_ref[r, start + 8 * i : start + 8 * i + 8, :], spot + 1, 1)
                out = jnp.where((lane == spot) | (lane == spot + 1), value, out)
        return out

    squeeze = jnp.minimum(lane + lane // 3, columns - 1)
    sublane = lax.broadcasted_iota(jnp.int32, (8, columns), 0)

    def tiles_of(j, r):
        start, count, _ = pieces[j]

        def tile_at(row):
            return z_ref[r, row : row + 8, :]

        if j < heat:
            return [tile_at(start + 8 * i) for i in range(count // 8)]
        out = [tile_at(start + half + 8 * i) for half in (0, pad) for i in range(full)]
        second = pltpu.roll(tile_at(start + pad + 8 * full), tail, 0)
        return out + [jnp.where(sublane < tail, tile_at(start + 8 * full), second)]

    def ship_rows(j):
        quads, width, height = packed[j]
        if j == 0:
            send(z_ref.at[distinct - 1, pl.ds(0, 1)], up_in.at[pl.ds(0, 1)], piece_sem.at[0], (f_dn, tile, lev))
            send(z_ref.at[0, pl.ds(0, 1)], down_in.at[pl.ds(0, 1)], piece_sem.at[0], (f_up, tile, lev))
            return
        at = first_row[j]
        for r, out, landing, to in (
            (distinct - 1, below, up_in, (f_dn, tile, lev)), (0, above_ref, down_in, (f_up, tile, lev))
        ):
            wide = tiles_of(j, r)
            thin = [jnp.take_along_axis(x, squeeze, axis=1) for x in wide]
            done = []
            for g in range(quads):
                spare = thin[4 * g + 3]
                for t in range(3):
                    done.append(jnp.where(
                        lane < 3 * quarter, thin[4 * g + t],
                        pltpu.roll(spare, (3 - t) * quarter, 1),
                    ))
            done += thin[4 * quads :]
            for i in range(4 * quads):
                spot = 3 * quarter + 1 + i
                done[-1] = jnp.where(
                    lane == spot, pltpu.roll(wide[i], (spot + 1) % columns, 1), done[-1]
                )
            for i, x in enumerate(done):
                out[at + 8 * i : at + 8 * i + 8, :] = x
            span = pl.ds(at, height)
            send(out.at[span], landing.at[span], piece_sem.at[j], to)

    def ship_sides(j):
        start, count, packs = pieces[j]
        each = count // packs
        made = []
        for p in range(packs):
            made.append(pack_of(start + p * each, each // 8))
            pack[first_pack[j] + p] = made[-1]
        span = pl.ds(first_pack[j], packs)
        for landing, to in ((left_in, (face, t_rt, lev)), (right_in, (face, t_lf, lev))):
            if j == 0:
                send(pack.at[0, pl.ds(0, 1)], landing.at[0, pl.ds(0, 1)], piece_sem.at[0], to)
            else:
                send(pack.at[span], landing.at[span], piece_sem.at[j], to)
        return made

    source = [unit - 2, unit - 1, 0, 1]

    def ship_corners(which, made):
        for d in range(4):
            out = jnp.zeros((8, columns), f32)
            for p, value in enumerate(made):
                out = jnp.where(within == p, pltpu.roll(value, (p - source[d]) % columns, 1), out)
            corner[which, d] = out
            part = pl.ds(0, 8 if which else 1)
            send(corner.at[which, d, part], corner_in.at[which, d, part],
                 corner_sem.at[which], diagonals[d])

    east = [level_rows(wind.at[0], a) for a in range(rows)]
    north = [level_rows(wind.at[1], a) for a in range(rows)]
    speed, parts = None, []
    whole = max(c[1] for c in chunks)
    for a in range(rows):
        aa = jac[a] * (m[0][a] * east[a] + m[1][a] * north[a])
        bb = jac[a] * (m[2][a] * east[a] + m[3][a] * north[a])
        parts.append(((aa * w_col)[:levels], (bb * wr[a])[:levels]))
        spacing = jnp.sqrt(
            m[0][a] * m[0][a] + m[1][a] * m[1][a] + m[2][a] * m[2][a] + m[3][a] * m[3][a]
        )
        here = jnp.max(east[a] * east[a] + north[a] * north[a], axis=0, keepdims=True)
        here = jnp.sqrt(here) * spacing
        speed = here if speed is None else jnp.maximum(speed, here)

    @pl.when(face < nf)
    def _():
        for a, pair in enumerate(parts):
            for k in range(-(-whole // levels)):
                n = min(levels, whole - k * levels)
                a_ref[a, k * levels : k * levels + n, :] = pair[0][:n]
                b_ref[a, k * levels : k * levels + n, :] = pair[1][:n]

    def tracers_of(k):
        start, count, _ = chunks[k]
        traced[k].wait()
        q = [tracer[pl.ds(start * rows + a, count, stride=rows), :] for a in range(rows)]
        first = [q[a] * a_ref[a, :count, :] for a in range(rows)]
        keep = [mass[a] * q[a] - along_rows(first, a, step_d[a]) for a in range(rows)]
        second = [q[a] * b_ref[a, :count, :] for a in range(rows)]
        for r, (x, y) in enumerate(zip(merged(keep), merged(second))):
            put(pieces[k + 1][0], 0, r, lanes_both(x, y))

    def tracers_ship(k):
        ship_rows(k + 1)
        return ship_sides(k + 1)

    tracers_of(0)
    pl.semaphore_wait(barrier, len(peers) + len(diagonals))
    made = tracers_ship(0)
    column_sums()
    for r, x in enumerate(merged(mass)):
        put(0, 0, r, lanes_plain(jnp.broadcast_to(x, (8, columns))))
    ship_rows(0)
    ship_corners(0, ship_sides(0))
    drain(group_rows[3], in_sem.at[3])
    depth = [level_rows(thick, a) for a in range(rows)]
    depth_c = by_column(depth)
    flux_a, flux_b = [], []
    for a in range(rows):
        dr, dc = along_rows(depth, a, dd[a % 4]), depth_c[a]
        gx, gy = m[0][a] * dr + m[2][a] * dc, m[1][a] * dr + m[3][a] * dc
        flux_a.append(jac[a] * (m[0][a] * gx + m[1][a] * gy))
        flux_b.append(jac[a] * (m[2][a] * gx + m[3][a] * gy))
    flux_c = by_column(flux_b)
    damp = None
    for a in range(rows):
        lap = jnp.abs(along_rows(flux_a, a, dd[a % 4]) + flux_c[a])
        here = jnp.max(lap, axis=0, keepdims=True) / jac[a]
        damp = here if damp is None else jnp.maximum(damp, here)
    peak[0] = jnp.concatenate(
        [time_step * speed, (time_step * viscosity) * damp, jnp.zeros((6, columns), f32)], 0
    )
    for o in range(1, nf):
        send(peak.at[0], peak_in.at[o - 1], peak_sem.at[0], (lax.rem(face + o, nf), tile, lev))

    early = min(3, len(chunks))
    for k in range(1, early):
        tracers_of(k)
        made += tracers_ship(k)

    first, second, keep = [], [], []
    for a in range(rows):
        aa = jac[a] * (m[0][a] * east[a] + m[1][a] * north[a])
        bb = jac[a] * (m[2][a] * east[a] + m[3][a] * north[a])
        first.append(w_col * (depth[a] * aa - viscosity * flux_a[a]))
        second.append(wr[a] * (depth[a] * bb - viscosity * flux_b[a]))
    for a in range(rows):
        keep.append(mass[a] * depth[a] - along_rows(first, a, step_d[a]))
    for r, (x, y) in enumerate(zip(merged(keep), merged(second))):
        put(pieces[heat][0], pad, r, lanes_both(x, y))
    warm = [level_rows(temp, a) for a in range(rows)]
    warm_c = by_column(warm)
    value = []
    for a in range(rows):
        dr, dc = along_rows(warm, a, dd[a % 4]), warm_c[a]
        gx, gy = m[0][a] * dr + m[2][a] * dc, m[1][a] * dr + m[3][a] * dc
        value.append(mass[a] * (warm[a] - time_step * (east[a] * gx + north[a] * gy)))
    for r, x in enumerate(merged(value)):
        put(pieces[heat][0], 0, r, lanes_plain(x))
    dynamic = ship_sides(heat)

    for k in range(early, len(chunks)):
        tracers_of(k)
        made += ship_sides(k + 1)
    ship_corners(1, made)

    above = ground[...]
    if nl > 1:
        drain((nl - 1) * rows, total_sem.at[0])
    for o in range(nl - 1):
        origin = lax.rem(lev + nl - (o + 1), nl)
        use = jnp.where(origin > lev, 1.0, 0.0).astype(f32)
        above = above + use * total_in[o]
    energy = []
    for a in range(rows):
        u, v = level_rows(wind.at[0], a), level_rows(wind.at[1], a)
        energy.append(0.5 * (u * u + v * v) + level_rows(geo, a) + above[a : a + 1, :])
    energy_c = by_column(energy)
    value_u, value_v = [], []
    for a in range(rows):
        u, v = level_rows(wind.at[0], a), level_rows(wind.at[1], a)
        dr, dc = along_rows(energy, a, dd[a % 4]), energy_c[a]
        value_u.append(mass[a] * (u - time_step * (m[0][a] * dr + m[2][a] * dc)))
        value_v.append(mass[a] * (v - time_step * (m[1][a] * dr + m[3][a] * dc)))
    for r, (x, y) in enumerate(zip(merged(value_u), merged(value_v))):
        put(pieces[last][0], 0, r, lanes_plain(x))
        put(pieces[last][0], pad, r, lanes_plain(y))
    dynamic += ship_sides(last)
    ship_corners(2, dynamic)
    ship_rows(last)
    for k in range(early, len(chunks)):
        ship_rows(k + 1)
    ship_rows(heat)

    def gathered(stage, base, count):
        best = peak[stage]
        if count:
            drain(8 * count, peak_sem.at[stage])
        for o in range(count):
            best = jnp.maximum(best, peak_in[base + o])
        return best

    def second_stage():
        peak[1] = gathered(0, 0, nf - 1)
        base = nf - 1
        for o in range(1, nt):
            send(peak.at[1], peak_in.at[base + o - 1], peak_sem.at[1],
                 (face, lax.rem(tile + o, nt), lev))

    def third_stage():
        peak[2] = gathered(1, nf - 1, nt - 1)
        base = nf + nt - 2
        for o in range(1, nl):
            send(peak.at[2], peak_in.at[base + o - 1], peak_sem.at[2],
                 (face, tile, lax.rem(lev + o, nl)))

    for load in tables:
        load.wait()

    def seam(ref, f, t, k):
        return ref[f, k, t]

    codes = [
        lax.rem(4 - seam(rot_ref, f_up, tile, 0), 4), seam(rot_ref, face, tile, 0),
        lax.rem(4 - seam(rot_ref, face, t_lf, 1), 4), seam(rot_ref, face, tile, 1),
    ]
    flips = [
        seam(flip_ref, f_up, tile, 0), seam(flip_ref, face, tile, 0),
        seam(flip_ref, face, t_lf, 1), seam(flip_ref, face, tile, 1),
    ]
    tallies = [
        tally_ref[f_up, t_lf], tally_ref[f_up, tile],
        tally_ref[face, t_lf], tally_ref[face, tile],
    ]

    def cosine(code):
        return jnp.where(code == 0, 1.0, jnp.where(code == 2, -1.0, 0.0)).astype(f32)

    def sine(code):
        return jnp.where(code == 1, 1.0, jnp.where(code == 3, -1.0, 0.0)).astype(f32)

    def filled(x):
        return jnp.full((8, columns), x)

    odd = lax.rem(lane, 2) == 1
    mirror = lane - within + (unit - 2) - 2 * (within // 2) + lax.rem(within, 2)
    mirror = jnp.clip(mirror, 0, columns - 1)
    side_flip = jnp.where(odd, filled(flips[2]), filled(flips[3])) == 1
    side_cos = jnp.where(odd, filled(cosine(codes[2])), filled(cosine(codes[3])))
    side_sin = jnp.where(odd, filled(sine(codes[2])), filled(sine(codes[3])))
    corner_code = [
        lax.rem(codes[0] + codes[2], 4), lax.rem(codes[0] + codes[3], 4),
        lax.rem(codes[1] + codes[2], 4), lax.rem(codes[1] + codes[3], 4),
    ]
    target = [1, 0, unit - 1, unit - 2]
    alive = [filled(tallies[d]) == 4 for d in range(4)]

    def sides(index):
        if index == 0:
            a = jnp.broadcast_to(left_in[0, 0:1, :], (8, columns))
            b = jnp.broadcast_to(right_in[0, 0:1, :], (8, columns))
        else:
            a, b = left_in[index], right_in[index]
        x = jnp.where(odd, pltpu.roll(a, 1, 1), pltpu.roll(b, columns - 1, 1))
        return jnp.where(side_flip, jnp.take_along_axis(x, mirror, axis=1), x)

    def corner_values(which, d, p):
        x = corner_in[which, d] if which else jnp.broadcast_to(corner_in[0, d, 0:1, :], (8, columns))
        x = pltpu.roll(x, (target[d] - p) % columns, 1)
        return jnp.where(alive[d] & (within == target[d]), x, 0.0)

    groups = pad // 8
    edge = (lane[:1] == 0) | (lane[:1] == columns - 1)

    def to_edges(x, i, r):
        y = pltpu.roll(x, (columns - (unit * i + 2 * r + 1)) % columns, 1)
        return jnp.where(edge, y, 0.0)

    rev = (columns - 1) - lane
    row_flip = [filled(flips[0]) == 1, filled(flips[1]) == 1]
    origin_lane = [jnp.where(row_flip[i], rev, lane) for i in range(2)]
    spread = [x - x // 4 for x in origin_lane]
    inner = [jnp.minimum(x, 3 * quarter - 1) for x in spread]
    rim_end = [x == columns - 1 for x in origin_lane]

    def row_rim(ref, which, j):
        if j == 0:
            x = jnp.broadcast_to(ref[0:1, :], (8, columns))
            return [jnp.take_along_axis(x, origin_lane[which], axis=1)]
        quads, width, _ = packed[j]
        at = first_row[j]
        got = [ref[at + 8 * i : at + 8 * i + 8, :] for i in range(width)]
        ends = got[-1]
        out = []
        for g in range(quads):
            one, two, three = got[3 * g : 3 * g + 3]
            four = jnp.where(
                lane < quarter, pltpu.roll(one, quarter, 1),
                jnp.where(lane < 2 * quarter, pltpu.roll(two, 2 * quarter, 1),
                          pltpu.roll(three, 3 * quarter, 1)),
            )
            for x in (one, two, three, four):
                spot = 3 * quarter + 1 + len(out)
                x = jnp.take_along_axis(x, inner[which], axis=1)
                end = jnp.broadcast_to(ends[:, spot : spot + 1], (8, columns))
                out.append(jnp.where(rim_end[which], end, x))
        for x in got[3 * quads :]:
            out.append(jnp.take_along_axis(x, spread[which], axis=1))
        if j >= heat:
            second = pltpu.roll(out[-1], 8 - tail, 0)
            out = out[:full] + out[-1:] + out[full : 2 * full] + [second]
        return out

    def arrived(j, corners=None):
        drain(2 * packed[j][2] + 2 * side_rows[j], piece_sem.at[j])
        if corners is not None:
            drain(4 * (8 if corners else 1), corner_sem.at[corners])

    def finished(start, i, r, side, i_side, top, bottom):
        x = z_ref[r, start + 8 * i : start + 8 * i + 8, :] + to_edges(side, i_side, r)
        if r == 0:
            x = x + top
        if r == distinct - 1:
            x = x + bottom
        return x

    def store(ref, begin, i, valid, r, x):
        n = min(8, valid - 8 * i)
        if n <= 0:
            return
        for a in range(rows):
            if rep[a] == r:
                ref[pl.ds((begin + 8 * i) * rows + a, n, stride=rows), :] = (x * inverse[a])[:n]

    arrived(0, 0)
    x = sides(0)
    for d in range(4):
        x = x + corner_values(0, d, 0)
    top, bottom = row_rim(up_in, 0, 0), row_rim(down_in, 1, 0)
    inverse = [None] * rows
    for r in range(distinct):
        whole_mass = 1.0 / finished(0, 0, r, x, 0, top[0], bottom[0])
        for a in range(rows):
            if rep[a] == r:
                inverse[a] = whole_mass

    def finish_tracers(k):
        start, count, valid = chunks[k]
        j = k + 1
        arrived(j, 1 if k == 0 else None)
        x = sides(first_pack[j])
        for d in range(4):
            x = x + corner_values(1, d, k)
        top = row_rim(up_in, 0, j)
        bottom = row_rim(down_in, 1, j)
        for i in range(count // 8):
            for r in range(distinct):
                store(tracer_o, start, i, valid, r,
                      finished(pieces[j][0], i, r, x, i, top[i], bottom[i]))

    second_stage()
    finish_tracers(0)
    for k in range(1, early):
        finish_tracers(k)
    third_stage()

    arrived(last, 2)
    p = first_pack[last]
    xu, xv = sides(p), sides(p + 1)
    xu, xv = side_cos * xu - side_sin * xv, side_sin * xu + side_cos * xv
    for d in range(4):
        cu, cv = corner_values(2, d, 1), corner_values(2, d, 2)
        c, s = cosine(corner_code[d]), sine(corner_code[d])
        xu, xv = xu + (c * cu - s * cv), xv + (s * cu + c * cv)
    begin = pieces[last][0]
    rims = []
    for which, ref in ((0, up_in), (1, down_in)):
        both = row_rim(ref, which, last)
        c, s = cosine(codes[which]), sine(codes[which])
        ru = [c * both[i] - s * both[groups + i] for i in range(groups)]
        rv = [s * both[i] + c * both[groups + i] for i in range(groups)]
        rims.append((ru, rv))
    for i in range(groups):
        for r in range(distinct):
            store(wind_o.at[0], 0, i, levels, r,
                  finished(begin, i, r, xu, i, rims[0][0][i], rims[1][0][i]))
            store(wind_o.at[1], 0, i, levels, r,
                  finished(begin + pad, i, r, xv, i, rims[0][1][i], rims[1][1][i]))

    for k in range(early, len(chunks)):
        finish_tracers(k)

    arrived(heat)
    begin = pieces[heat][0]
    x = sides(first_pack[heat])
    for d in range(4):
        x = x + corner_values(2, d, 0)
    top, bottom = row_rim(up_in, 0, heat), row_rim(down_in, 1, heat)
    for i in range(groups):
        for r in range(distinct):
            store(temp_o, 0, i, levels, r, finished(begin, i, r, x, i, top[i], bottom[i]))
            j = groups + i
            store(thick_o, 0, i, levels, r, finished(begin, j, r, x, j, top[j], bottom[j]))

    bound_o[...] = gathered(2, nf + nt - 2, nl - 1)
    drain(sum(sent), sent_sem.at[0])


def write_out(wind, temp, thick, tracer, bound, wind_o, temp_o, thick_o, tracer_o, bound_o, sem):
    pairs = ((tracer, tracer_o), (wind, wind_o), (temp, temp_o), (thick, thick_o))
    copies = [pltpu.make_async_copy(a, b, sem.at[i]) for i, (a, b) in enumerate(pairs)]
    for copy in copies:
        copy.start()
    bound_o[0] = jnp.max(bound[0:1, :])
    bound_o[1] = jnp.max(bound[1:2, :])
    for copy in copies:
        copy.wait()


def on_device(
    sizes, wind, temp, thick, tracers, ground, maps, det, rot, flip, tally
):
    nf, nt, nl = sizes
    levels, rows, columns = temp.shape
    if rows != 8 or columns != 128 or levels % 8 not in (1, 2, 3, 4):
        raise ValueError("block shape")
    count = tracers.shape[0]
    chunks = layout(levels, count)
    pad = -(-levels // 8) * 8
    table, dct, w_col = lane_tables(columns)
    distinct = rows - rows // 4 + 1
    total_rows = 4 * pad + 8 + sum(c[1] for c in chunks)
    pieces = len(chunks) + 3
    packs = len(chunks) + 4
    landing = sum(8 * p[1] for p in packing(levels, chunks))
    whole = max(c[1] for c in chunks)
    n = levels * rows
    dma = pltpu.SemaphoreType.DMA
    peers = nf + nt + nl - 3
    hbm = pl.BlockSpec(memory_space=pl.ANY)
    smem = pl.BlockSpec(memory_space=pltpu.SMEM)
    vmem = pl.BlockSpec(memory_space=pltpu.VMEM)
    last = chunks[-1]
    shapes = ((2, n, columns), (n, columns), (n, columns), (count * n, columns), (8, columns))
    outs = pl.pallas_call(
        functools.partial(kernel, sizes, (levels, rows, columns, chunks, pad)),
        out_shape=tuple(pltpu.VMEM(shape, f32) for shape in shapes),
        in_specs=[hbm] * 13,
        out_specs=(vmem,) * 5,
        scratch_shapes=[
            pltpu.VMEM((2, pad * rows, columns), f32),
            pltpu.VMEM((pad * rows, columns), f32),
            pltpu.VMEM((pad * rows, columns), f32),
            pltpu.VMEM(((last[0] + last[1]) * rows, columns), f32),
            pltpu.VMEM((pad * rows, columns), f32),
            pltpu.VMEM((rows, columns), f32),
            pltpu.VMEM((4 * rows, columns), f32),
            pltpu.VMEM((rows, columns), f32),
            pltpu.VMEM(table.shape, bf16),
            pltpu.VMEM(dct.shape, bf16),
            pltpu.VMEM((1, columns), f32),
            pltpu.VMEM((rows, whole, columns), f32),
            pltpu.VMEM((rows, whole, columns), f32),
            pltpu.VMEM((distinct, total_rows, columns), f32),
            pltpu.VMEM((landing, columns), f32),
            pltpu.VMEM((landing, columns), f32),
            pltpu.VMEM((packs, 8, columns), f32),
            pltpu.VMEM((3, 4, 8, columns), f32),
            pltpu.VMEM((rows, columns), f32),
            pltpu.VMEM((3, 8, columns), f32),
            pltpu.VMEM((landing, columns), f32),
            pltpu.VMEM((landing, columns), f32),
            pltpu.VMEM((packs, 8, columns), f32),
            pltpu.VMEM((packs, 8, columns), f32),
            pltpu.VMEM((3, 4, 8, columns), f32),
            pltpu.VMEM((nl - 1, rows, columns), f32),
            pltpu.VMEM((peers, 8, columns), f32),
            pltpu.SMEM((nf, 2, nt), jnp.int32),
            pltpu.SMEM((nf, 2, nt), jnp.int32),
            pltpu.SMEM((nf, nt), jnp.int32),
            dma((7 + len(chunks),)),
            dma((1,)),
            dma((pieces,)),
            dma((3,)),
            dma((1,)),
            dma((3,)),
        ],
        compiler_params=pltpu.CompilerParams(collective_id=0, has_side_effects=True),
    )(
        wind.reshape(2, n, columns), temp.reshape(n, columns), thick.reshape(n, columns),
        tracers.reshape(count * n, columns), ground, maps.reshape(4 * rows, columns), det,
        table, dct, w_col, rot.transpose(0, 2, 1), flip.transpose(0, 2, 1), tally,
    )
    outs = pl.pallas_call(
        write_out,
        out_shape=tuple(jax.ShapeDtypeStruct(x, f32) for x in shapes[:4] + ((2,),)),
        in_specs=[vmem] * 5,
        out_specs=(hbm,) * 4 + (smem,),
        scratch_shapes=[dma((4,))],
    )(*[pltpu.with_memory_space_constraint(x, pltpu.VMEM) for x in outs])
    return (
        outs[0].reshape(wind.shape), outs[1].reshape(temp.shape), outs[2].reshape(thick.shape),
        outs[3].reshape(tracers.shape), outs[4],
    )


def solution(mesh):
    sizes = tuple(mesh.shape[name] for name in ("face", "tile", "lev"))
    level = P("lev", "face", "tile")
    stacked = P(None, "lev", "face", "tile")
    return jax.shard_map(
        functools.partial(on_device, sizes),
        mesh=mesh,
        in_specs=(stacked, level, level, stacked, P("face", "tile"), P(None, "face", "tile"),
                  P("face", "tile"), P(), P(), P()),
        out_specs=(stacked, level, level, stacked, P()),
        check_vma=False,
    )
```

profile of v0, /device:TPU:0, one launch (start us, length us, event | category | flops | bytes accessed | tf_op | source)
XLA Modules:
  0.0 20.1 jit_solution(4166742891334534430)
XLA Ops:
  0.6 17.8 %shard_map.173 = (f32[2,144,128]{2,1,0:T(8,128)S(1)}, f32[144,128]{1,0:T(8,128)S(1)}, f32[144,128]{1,0:T(8,128)S(1)}, f32[2592,128]{1,0:T(8,128)S(1)}, f32[8,128]{1,0:T(8,128)S(1)}) custom-call(f32[2,144,128]{2,1,0:T(8,128)} %bitcast.12, f32[144,128]{1,0:T(8,128)} %bitcast.13, f32[144,128]{1,0:T(8,128)} %bitcast.14, f32[2592,128]{1,0:T(8,128)} %bitcast.11, ...), custom_call_target="tpu_custom_call" | custom-call | tf_op jit(solution)/shard_map/pallas_call | solution.py:706
  18.4 1.7 %shard_map.174 = (f32[2,144,128]{2,1,0:T(8,128)}, f32[144,128]{1,0:T(8,128)}, f32[144,128]{1,0:T(8,128)}, f32[2592,128]{1,0:T(8,128)}, f32[2]{0:T(128)}) custom-call(f32[2,144,128]{2,1,0:T(8,128)S(1)} %get-tuple-element.15.wind, f32[144,128]{1,0:T(8,128)S(1)} %get-tuple-element.16.temp, f32[144,128]{1,0:T(8,128)S(1)} %get-tuple-element.17.thick, ...), custom_call_target="tpu_custom_call" | custom-call | tf_op jit(solution)/shard_map/pallas_call | solution.py:755
where the time goes:
time: 20.2 us; the launch traced here: 20.1 us
  Pallas kernels  19.5 us (97%)
  between operations  0.64 us (3%)
    pallas_call x1, Pallas kernels, on_device(): pl.pallas_call(functools.partial(kernel, sizes, (levels, rows, columns, c...  17.8 us
    pallas_call x1, Pallas kernels, on_device(): pl.pallas_call(write_out, out_shape=tuple((jax.ShapeDtypeStruct(x, f32) f...  1.7 us

commit v1 on v0

--- a/solution.py
+++ b/solution.py
@@ -82,10 +82,10 @@
     rot_h, flip_h, tally_h,
     wind_o, temp_o, thick_o, tracer_o, bound_o,
     wind, temp, thick, tracer, geo, ground, maps, det, ops, dct, wc,
-    a_ref, b_ref, z_ref, below, above_ref, pack, corner, total, peak,
+    a_ref, b_ref, z_ref, below, above_ref, pack, seam_x, corner, total, peak,
     up_in, down_in, left_in, right_in, corner_in, total_in, peak_in,
     rot_ref, flip_ref, tally_ref,
-    in_sem, sent_sem, piece_sem, corner_sem, total_sem, peak_sem,
+    in_sem, sent_sem, piece_sem, side_sem, corner_sem, total_sem, peak_sem, chain_sem,
 ):
     nf, nt, nl = sizes
     levels, rows, columns, chunks, pad = dims
@@ -149,13 +149,71 @@
     for load in tables:
         load.start()
 
-    peers = [(lax.rem(face + o, nf), tile, lev) for o in range(1, nf)]
-    peers += [(face, lax.rem(tile + o, nt), lev) for o in range(1, nt)]
-    peers += [(face, tile, lax.rem(lev + o, nl)) for o in range(1, nl)]
     diagonals = [(f_dn, t_rt, lev), (f_dn, t_lf, lev), (f_up, t_rt, lev), (f_up, t_lf, lev)]
     barrier = pltpu.get_barrier_semaphore()
-    for peer in peers + diagonals:
-        pl.semaphore_signal(barrier, inc=1, device_id=peer, device_id_type=MESH)
+
+    def notify(sem, to):
+        pl.semaphore_signal(sem, inc=1, device_id=to, device_id_type=MESH)
+
+    has_up, has_dn = face > 0, face < nf - 1
+    at_end = face == nf - 1
+    plane = [
+        (face, lax.rem(tile + o, nt), lax.rem(lev + p, nl))
+        for o in range(nt) for p in range(nl) if o or p
+    ]
+
+    def one(flag):
+        return jnp.where(flag, 1, 0)
+
+    for o in range(nf - 1, 1, -1):
+        @pl.when(face + o < nf)
+        def _():
+            notify(barrier, (face + o, tile, lev))
+    for here, other in ((has_up, face - 1), (has_dn, face + 1)):
+        @pl.when(here)
+        def _():
+            for t in (tile, t_lf, t_rt):
+                notify(barrier, (other, t, lev))
+
+    @pl.when(face == 0)
+    def _():
+        for t in (t_lf, t_rt):
+            notify(barrier, (nf - 1, t, lev))
+    for o in range(nt):
+        for p in range(nl):
+            if o and p:
+                @pl.when(tile + o < nt)
+                def _():
+                    notify(barrier, (face, tile + o, lax.rem(lev + p, nl)))
+            elif o or p:
+                notify(barrier, (face, lax.rem(tile + o, nt), lax.rem(lev + p, nl)))
+    known = (
+        nt - 1 + (nl - 1) * (1 + tile) + face + one(has_dn)
+        + 2 * (one(has_up) + one(has_dn) + one(at_end))
+    )
+    unknown = (nt - 1 - tile) * (nl - 1) + jnp.maximum(nf - 2 - face, 0) + 2 * one(face == 0)
+
+    def enter():
+        pl.semaphore_wait(barrier, known)
+        for o in range(2, nf):
+            @pl.when(face - o >= 0)
+            def _():
+                notify(chain_sem.at[0], (face - o, tile, lev))
+
+        @pl.when(at_end)
+        def _():
+            for t in (t_lf, t_rt):
+                notify(chain_sem.at[0], (0, t, lev))
+        for o in range(1, nt):
+            for p in range(1, nl):
+                @pl.when(tile - o >= 0)
+                def _():
+                    notify(chain_sem.at[0], (face, tile - o, lax.rem(lev + p, nl)))
+
+    def ends_meet():
+        @pl.when(unknown > 0)
+        def _():
+            pl.semaphore_wait(chain_sem.at[0], unknown)
 
     extra = (pad - levels) * rows
     if extra:
@@ -180,13 +238,14 @@
         sent.append(math.prod(src.shape) // columns)
 
     def column_sums():
-        drain(group_rows[1], in_sem.at[1])
         acc = jnp.zeros((rows, columns), f32)
         for k in reversed(range(levels)):
             term = temp[k * rows : (k + 1) * rows, :] * thick[k * rows : (k + 1) * rows, :]
             geo[k * rows : (k + 1) * rows, :] = acc + 0.5 * term
             acc = acc + term
         total[...] = acc
+
+    def send_totals():
         for o in range(1, nl):
             send(total, total_in.at[o - 1], total_sem.at[0], (face, tile, lax.rem(lev + o, nl)))
 
@@ -270,16 +329,10 @@
         second = pltpu.roll(tile_at(start + pad + 8 * full), tail, 0)
         return out + [jnp.where(sublane < tail, tile_at(start + 8 * full), second)]
 
-    def ship_rows(j):
-        quads, width, height = packed[j]
-        if j == 0:
-            send(z_ref.at[distinct - 1, pl.ds(0, 1)], up_in.at[pl.ds(0, 1)], piece_sem.at[0], (f_dn, tile, lev))
-            send(z_ref.at[0, pl.ds(0, 1)], down_in.at[pl.ds(0, 1)], piece_sem.at[0], (f_up, tile, lev))
-            return
+    def squeeze_rows(j):
+        quads = packed[j][0]
         at = first_row[j]
-        for r, out, landing, to in (
-            (distinct - 1, below, up_in, (f_dn, tile, lev)), (0, above_ref, down_in, (f_up, tile, lev))
-        ):
+        for r, out in ((distinct - 1, below), (0, above_ref)):
             wide = tiles_of(j, r)
             thin = [jnp.take_along_axis(x, squeeze, axis=1) for x in wide]
             done = []
@@ -298,33 +351,67 @@
                 )
             for i, x in enumerate(done):
                 out[at + 8 * i : at + 8 * i + 8, :] = x
-            span = pl.ds(at, height)
-            send(out.at[span], landing.at[span], piece_sem.at[j], to)
-
-    def ship_sides(j):
+
+    def row_copy(j, down):
+        height = packed[j][2]
+        if j == 0:
+            span = pl.ds(0, 1)
+            source = z_ref.at[distinct - 1 if down else 0, span]
+        else:
+            span = pl.ds(first_row[j], height)
+            source = (below if down else above_ref).at[span]
+        landing = up_in if down else down_in
+        send(source, landing.at[span], piece_sem.at[j], (f_dn if down else f_up, tile, lev))
+
+    def ship_near(j):
+        row_copy(j, True)
+
+        @pl.when(has_up)
+        def _():
+            row_copy(j, False)
+        sent.pop()
+
+    def ship_wrap(j):
+        @pl.when(face == 0)
+        def _():
+            row_copy(j, False)
+
+    def ship_rows(j):
+        row_copy(j, True)
+        row_copy(j, False)
+
+    def pack_sides(j):
         start, count, packs = pieces[j]
         each = count // packs
         made = []
         for p in range(packs):
             made.append(pack_of(start + p * each, each // 8))
             pack[first_pack[j] + p] = made[-1]
-        span = pl.ds(first_pack[j], packs)
+        return made
+
+    def ship_sides(j):
+        span = pl.ds(first_pack[j], pieces[j][2])
         for landing, to in ((left_in, (face, t_rt, lev)), (right_in, (face, t_lf, lev))):
             if j == 0:
-                send(pack.at[0, pl.ds(0, 1)], landing.at[0, pl.ds(0, 1)], piece_sem.at[0], to)
+                send(pack.at[0, pl.ds(0, 1)], landing.at[0, pl.ds(0, 1)], side_sem.at[0], to)
             else:
-                send(pack.at[span], landing.at[span], piece_sem.at[j], to)
-        return made
+                send(pack.at[span], landing.at[span], side_sem.at[j], to)
 
     source = [unit - 2, unit - 1, 0, 1]
 
-    def ship_corners(which, made):
+    def pack_corners(which, made):
         for d in range(4):
             out = jnp.zeros((8, columns), f32)
             for p, value in enumerate(made):
                 out = jnp.where(within == p, pltpu.roll(value, (p - source[d]) % columns, 1), out)
+            if which:
+                folded = pltpu.roll(pltpu.roll(out, 4, 0), unit // 2, 1)
+                out = jnp.where(within < unit // 2, out, folded)
             corner[which, d] = out
-            part = pl.ds(0, 8 if which else 1)
+
+    def ship_corners(which):
+        part = pl.ds(0, 4 if which else 1)
+        for d in range(4):
             send(corner.at[which, d, part], corner_in.at[which, d, part],
                  corner_sem.at[which], diagonals[d])
 
@@ -351,9 +438,15 @@
                 a_ref[a, k * levels : k * levels + n, :] = pair[0][:n]
                 b_ref[a, k * levels : k * levels + n, :] = pair[1][:n]
 
+    def put_mass():
+        whole_rows = lanes_plain(jnp.concatenate(
+            [jnp.broadcast_to(x, (8, columns)) for x in merged(mass)], 0
+        ))
+        for r in range(distinct):
+            put(0, 0, r, whole_rows[8 * r : 8 * r + 8])
+
     def tracers_of(k):
         start, count, _ = chunks[k]
-        traced[k].wait()
         q = [tracer[pl.ds(start * rows + a, count, stride=rows), :] for a in range(rows)]
         first = [q[a] * a_ref[a, :count, :] for a in range(rows)]
         keep = [mass[a] * q[a] - along_rows(first, a, step_d[a]) for a in range(rows)]
@@ -361,19 +454,35 @@
         for r, (x, y) in enumerate(zip(merged(keep), merged(second))):
             put(pieces[k + 1][0], 0, r, lanes_both(x, y))
 
-    def tracers_ship(k):
-        ship_rows(k + 1)
-        return ship_sides(k + 1)
-
+
+    def ready(j):
+        squeeze_rows(j)
+        return pack_sides(j)
+
+    traced[0].wait()
     tracers_of(0)
-    pl.semaphore_wait(barrier, len(peers) + len(diagonals))
-    made = tracers_ship(0)
+    made = ready(1)
+    enter()
+    ship_near(1)
+    ship_sides(1)
+
+    drain(group_rows[1], in_sem.at[1])
+    traced[1].wait()
     column_sums()
-    for r, x in enumerate(merged(mass)):
-        put(0, 0, r, lanes_plain(jnp.broadcast_to(x, (8, columns))))
-    ship_rows(0)
-    ship_corners(0, ship_sides(0))
+    put_mass()
+    tracers_of(1)
+    mass_made = pack_sides(0)
+    pack_corners(0, mass_made)
+    made += ready(2)
+    send_totals()
+    ship_near(2)
+    ship_sides(2)
+    ship_near(0)
+    ship_sides(0)
+
     drain(group_rows[3], in_sem.at[3])
+    traced[2].wait()
+    tracers_of(2)
     depth = [level_rows(thick, a) for a in range(rows)]
     depth_c = by_column(depth)
     flux_a, flux_b = [], []
@@ -391,14 +500,6 @@
     peak[0] = jnp.concatenate(
         [time_step * speed, (time_step * viscosity) * damp, jnp.zeros((6, columns), f32)], 0
     )
-    for o in range(1, nf):
-        send(peak.at[0], peak_in.at[o - 1], peak_sem.at[0], (lax.rem(face + o, nf), tile, lev))
-
-    early = min(3, len(chunks))
-    for k in range(1, early):
-        tracers_of(k)
-        made += tracers_ship(k)
-
     first, second, keep = [], [], []
     for a in range(rows):
         aa = jac[a] * (m[0][a] * east[a] + m[1][a] * north[a])
@@ -418,16 +519,31 @@
         value.append(mass[a] * (warm[a] - time_step * (east[a] * gx + north[a] * gy)))
     for r, x in enumerate(merged(value)):
         put(pieces[heat][0], 0, r, lanes_plain(x))
-    dynamic = ship_sides(heat)
-
-    for k in range(early, len(chunks)):
-        tracers_of(k)
-        made += ship_sides(k + 1)
-    ship_corners(1, made)
-
-    above = ground[...]
+    made += ready(3)
+    made += ready(heat)
+    ship_near(3)
+    ship_sides(3)
+    ship_near(heat)
+    ship_sides(heat)
+
+    traced[3].wait()
+    tracers_of(3)
+    pack_corners(1, made)
+    later = ready(4)
+    ends_meet()
+    ship_corners(0)
+    for o, peer in enumerate(plane):
+        send(peak.at[0, pl.ds(0, 2)], peak_in.at[o, pl.ds(0, 2)], peak_sem.at[0], peer)
+    ship_near(4)
+    ship_sides(4)
+    ship_corners(1)
+    for j in (0, 1, 2, 3, heat, 4):
+        ship_wrap(j)
+
     if nl > 1:
         drain((nl - 1) * rows, total_sem.at[0])
+    traced[4].wait()
+    above = ground[...]
     for o in range(nl - 1):
         origin = lax.rem(lev + nl - (o + 1), nl)
         use = jnp.where(origin > lev, 1.0, 0.0).astype(f32)
@@ -446,34 +562,36 @@
     for r, (x, y) in enumerate(zip(merged(value_u), merged(value_v))):
         put(pieces[last][0], 0, r, lanes_plain(x))
         put(pieces[last][0], pad, r, lanes_plain(y))
-    dynamic += ship_sides(last)
-    ship_corners(2, dynamic)
+    tracers_of(4)
+    later += ready(last)
+    later += ready(5)
+    pack_corners(2, later)
+    ship_sides(last)
+    ship_sides(5)
+    ship_corners(2)
     ship_rows(last)
-    for k in range(early, len(chunks)):
-        ship_rows(k + 1)
-    ship_rows(heat)
+    ship_rows(5)
+
+    def spread_peaks():
+        best = peak[0]
+        if plane:
+            drain(2 * len(plane), peak_sem.at[0])
+        for o in range(len(plane)):
+            best = jnp.maximum(best, peak_in[o])
+        peak[1] = best
+        for o in range(1, nf):
+            send(peak.at[1, pl.ds(0, 2)], peak_in.at[len(plane) + o - 1, pl.ds(0, 2)],
+                 peak_sem.at[1], (lax.rem(face + o, nf), tile, lev))
+
+    spread_peaks()
 
     def gathered(stage, base, count):
         best = peak[stage]
         if count:
-            drain(8 * count, peak_sem.at[stage])
+            drain(2 * count, peak_sem.at[stage])
         for o in range(count):
             best = jnp.maximum(best, peak_in[base + o])
         return best
-
-    def second_stage():
-        peak[1] = gathered(0, 0, nf - 1)
-        base = nf - 1
-        for o in range(1, nt):
-            send(peak.at[1], peak_in.at[base + o - 1], peak_sem.at[1],
-                 (face, lax.rem(tile + o, nt), lev))
-
-    def third_stage():
-        peak[2] = gathered(1, nf - 1, nt - 1)
-        base = nf + nt - 2
-        for o in range(1, nl):
-            send(peak.at[2], peak_in.at[base + o - 1], peak_sem.at[2],
-                 (face, tile, lax.rem(lev + o, nl)))
 
     for load in tables:
         load.wait()
@@ -525,12 +643,18 @@
         x = jnp.where(odd, pltpu.roll(a, 1, 1), pltpu.roll(b, columns - 1, 1))
         return jnp.where(side_flip, jnp.take_along_axis(x, mirror, axis=1), x)
 
+    def corner_tile(which, d):
+        if which == 0:
+            return jnp.broadcast_to(corner_in[0, d, 0:1, :], (8, columns))
+        x = corner_in[which, d]
+        lower = pltpu.roll(pltpu.roll(x, 4, 0), columns - unit // 2, 1)
+        return jnp.where(sublane < 4, x, lower)
+
     def corner_values(which, d, p):
-        x = corner_in[which, d] if which else jnp.broadcast_to(corner_in[0, d, 0:1, :], (8, columns))
+        x = corner_tile(which, d)
         x = pltpu.roll(x, (target[d] - p) % columns, 1)
         return jnp.where(alive[d] & (within == target[d]), x, 0.0)
 
-    groups = pad // 8
     edge = (lane[:1] == 0) | (lane[:1] == columns - 1)
 
     def to_edges(x, i, r):
@@ -572,98 +696,94 @@
             out = out[:full] + out[-1:] + out[full : 2 * full] + [second]
         return out
 
-    def arrived(j, corners=None):
-        drain(2 * packed[j][2] + 2 * side_rows[j], piece_sem.at[j])
-        if corners is not None:
-            drain(4 * (8 if corners else 1), corner_sem.at[corners])
-
-    def finished(start, i, r, side, i_side, top, bottom):
-        x = z_ref[r, start + 8 * i : start + 8 * i + 8, :] + to_edges(side, i_side, r)
-        if r == 0:
-            x = x + top
-        if r == distinct - 1:
-            x = x + bottom
-        return x
-
-    def store(ref, begin, i, valid, r, x):
+    sets = [[0], [1, 2, 3, heat], [4, last, last, 5]]
+    corner_spot = {j: (w, group.index(j)) for w, group in enumerate(sets) for j in group}
+
+    def sides_of(j):
+        p = first_pack[j]
+        if j < last:
+            return [sides(p)]
+        xu, xv = sides(p), sides(p + 1)
+        return [side_cos * xu - side_sin * xv, side_sin * xu + side_cos * xv]
+
+    def with_corners(j):
+        which, p = corner_spot[j]
+        if j < last:
+            return [seam_x[first_pack[j]] + sum_corners(which, p)]
+        xu, xv = seam_x[first_pack[j]], seam_x[first_pack[j] + 1]
+        for d in range(4):
+            cu, cv = corner_values(which, d, p), corner_values(which, d, p + 1)
+            c, s = cosine(corner_code[d]), sine(corner_code[d])
+            xu, xv = xu + (c * cu - s * cv), xv + (s * cu + c * cv)
+        return [xu, xv]
+
+    def sum_corners(which, p):
+        parts = [corner_values(which, d, p) for d in range(4)]
+        return parts[0] + parts[1] + parts[2] + parts[3]
+
+    def rims_of(j):
+        both = [row_rim(up_in, 0, j), row_rim(down_in, 1, j)]
+        if j == last:
+            for which in range(2):
+                x = both[which]
+                c, s = cosine(codes[which]), sine(codes[which])
+                ru = [c * x[i] - s * x[groups + i] for i in range(groups)]
+                rv = [s * x[i] + c * x[groups + i] for i in range(groups)]
+                both[which] = ru + rv
+        return both
+
+    def stored(ref, begin, i, valid, r, x):
         n = min(8, valid - 8 * i)
-        if n <= 0:
-            return
         for a in range(rows):
             if rep[a] == r:
                 ref[pl.ds((begin + 8 * i) * rows + a, n, stride=rows), :] = (x * inverse[a])[:n]
 
-    arrived(0, 0)
-    x = sides(0)
-    for d in range(4):
-        x = x + corner_values(0, d, 0)
-    top, bottom = row_rim(up_in, 0, 0), row_rim(down_in, 1, 0)
     inverse = [None] * rows
-    for r in range(distinct):
-        whole_mass = 1.0 / finished(0, 0, r, x, 0, top[0], bottom[0])
-        for a in range(rows):
-            if rep[a] == r:
-                inverse[a] = whole_mass
-
-    def finish_tracers(k):
-        start, count, valid = chunks[k]
-        j = k + 1
-        arrived(j, 1 if k == 0 else None)
-        x = sides(first_pack[j])
-        for d in range(4):
-            x = x + corner_values(1, d, k)
-        top = row_rim(up_in, 0, j)
-        bottom = row_rim(down_in, 1, j)
-        for i in range(count // 8):
-            for r in range(distinct):
-                store(tracer_o, start, i, valid, r,
-                      finished(pieces[j][0], i, r, x, i, top[i], bottom[i]))
-
-    second_stage()
-    finish_tracers(0)
-    for k in range(1, early):
-        finish_tracers(k)
-    third_stage()
-
-    arrived(last, 2)
-    p = first_pack[last]
-    xu, xv = sides(p), sides(p + 1)
-    xu, xv = side_cos * xu - side_sin * xv, side_sin * xu + side_cos * xv
-    for d in range(4):
-        cu, cv = corner_values(2, d, 1), corner_values(2, d, 2)
-        c, s = cosine(corner_code[d]), sine(corner_code[d])
-        xu, xv = xu + (c * cu - s * cv), xv + (s * cu + c * cv)
-    begin = pieces[last][0]
-    rims = []
-    for which, ref in ((0, up_in), (1, down_in)):
-        both = row_rim(ref, which, last)
-        c, s = cosine(codes[which]), sine(codes[which])
-        ru = [c * both[i] - s * both[groups + i] for i in range(groups)]
-        rv = [s * both[i] + c * both[groups + i] for i in range(groups)]
-        rims.append((ru, rv))
-    for i in range(groups):
-        for r in range(distinct):
-            store(wind_o.at[0], 0, i, levels, r,
-                  finished(begin, i, r, xu, i, rims[0][0][i], rims[1][0][i]))
-            store(wind_o.at[1], 0, i, levels, r,
-                  finished(begin + pad, i, r, xv, i, rims[0][1][i], rims[1][1][i]))
-
-    for k in range(early, len(chunks)):
-        finish_tracers(k)
-
-    arrived(heat)
-    begin = pieces[heat][0]
-    x = sides(first_pack[heat])
-    for d in range(4):
-        x = x + corner_values(2, d, 0)
-    top, bottom = row_rim(up_in, 0, heat), row_rim(down_in, 1, heat)
-    for i in range(groups):
-        for r in range(distinct):
-            store(temp_o, 0, i, levels, r, finished(begin, i, r, x, i, top[i], bottom[i]))
-            j = groups + i
-            store(thick_o, 0, i, levels, r, finished(begin, j, r, x, j, top[j], bottom[j]))
-
-    bound_o[...] = gathered(2, nf + nt - 2, nl - 1)
+    insides, borders = range(1, distinct - 1), (0, distinct - 1)
+
+    def finish(j, seams, which_rows, both=None):
+        start, total_count, packs = pieces[j]
+        each = (total_count // packs) // 8
+        for i in range(total_count // 8):
+            for r in which_rows:
+                x = z_ref[r, start + 8 * i : start + 8 * i + 8, :]
+                x = x + to_edges(seams[i // each], i % each, r)
+                if r in borders:
+                    x = x + both[0 if r == 0 else 1][i]
+                if j == 0:
+                    for a in range(rows):
+                        if rep[a] == r:
+                            inverse[a] = 1.0 / x
+                elif j < heat:
+                    begin, _, valid = chunks[j - 1]
+                    stored(tracer_o, begin, i, valid, r, x)
+                else:
+                    first_half, k = i < groups, i % groups
+                    if j == heat:
+                        ref = temp_o if first_half else thick_o
+                    else:
+                        ref = wind_o.at[0 if first_half else 1]
+                    stored(ref, 0, k, levels, r, x)
+
+    groups = pad // 8
+    order = [0, 1, 2, 3, heat, 4, last, 5]
+    for j in order:
+        drain(2 * side_rows[j], side_sem.at[j])
+    for j in order:
+        seams = sides_of(j)
+        for i, x in enumerate(seams):
+            seam_x[first_pack[j] + i] = x
+        finish(j, seams, insides)
+    for block in (sets[0] + sets[1], list(dict.fromkeys(sets[2]))):
+        for j in block:
+            drain(2 * packed[j][2], piece_sem.at[j])
+        if 0 in block:
+            drain(4, corner_sem.at[0])
+        drain(16, corner_sem.at[1 if 0 in block else 2])
+        for j in block:
+            finish(j, with_corners(j), borders, rims_of(j))
+
+    bound_o[...] = gathered(1, len(plane), nf - 1)
     drain(sum(sent), sent_sem.at[0])
 
 
@@ -683,11 +803,11 @@
 ):
     nf, nt, nl = sizes
     levels, rows, columns = temp.shape
-    if rows != 8 or columns != 128 or levels % 8 not in (1, 2, 3, 4):
-        raise ValueError("block shape")
     count = tracers.shape[0]
     chunks = layout(levels, count)
     pad = -(-levels // 8) * 8
+    if rows != 8 or columns != 128 or levels % 8 not in (1, 2, 3, 4) or len(chunks) != 5:
+        raise ValueError("block shape")
     table, dct, w_col = lane_tables(columns)
     distinct = rows - rows // 4 + 1
     total_rows = 4 * pad + 8 + sum(c[1] for c in chunks)
@@ -697,7 +817,7 @@
     whole = max(c[1] for c in chunks)
     n = levels * rows
     dma = pltpu.SemaphoreType.DMA
-    peers = nf + nt + nl - 3
+    peers = nt * nl - 1 + nf - 1
     hbm = pl.BlockSpec(memory_space=pl.ANY)
     smem = pl.BlockSpec(memory_space=pltpu.SMEM)
     vmem = pl.BlockSpec(memory_space=pltpu.VMEM)
@@ -726,9 +846,10 @@
             pltpu.VMEM((landing, columns), f32),
             pltpu.VMEM((landing, columns), f32),
             pltpu.VMEM((packs, 8, columns), f32),
+            pltpu.VMEM((packs, 8, columns), f32),
             pltpu.VMEM((3, 4, 8, columns), f32),
             pltpu.VMEM((rows, columns), f32),
-            pltpu.VMEM((3, 8, columns), f32),
+            pltpu.VMEM((2, 8, columns), f32),
             pltpu.VMEM((landing, columns), f32),
             pltpu.VMEM((landing, columns), f32),
             pltpu.VMEM((packs, 8, columns), f32),
@@ -742,9 +863,11 @@
             dma((7 + len(chunks),)),
             dma((1,)),
             dma((pieces,)),
+            dma((pieces,)),
             dma((3,)),
             dma((1,)),
-            dma((3,)),
+            dma((2,)),
+            pltpu.SemaphoreType.REGULAR((1,)),
         ],
         compiler_params=pltpu.CompilerParams(collective_id=0, has_side_effects=True),
     )(

time: 20.2 us -> 18.7 us (0.926)
  the two profiles are of different devices: /device:TPU:0 before, /device:TPU:1 now
where the time goes in v1:
time: 18.7 us; the launch traced here: 18.5 us
  Pallas kernels  17.9 us (96%)
  between operations  0.64 us (3%)
    pallas_call x1, Pallas kernels, on_device(): pl.pallas_call(functools.partial(kernel, sizes, (levels, rows, columns, c...  16.2 us
    pallas_call x1, Pallas kernels, on_device(): pl.pallas_call(write_out, out_shape=tuple((jax.ShapeDtypeStruct(x, f32) f...  1.7 us

profile of v1, /device:TPU:1, one launch (start us, length us, event | category | flops | bytes accessed | tf_op | source)
XLA Modules:
  0.0 18.5 jit_solution(10818289233106363754)
XLA Ops:
  0.6 16.2 %shard_map.173 = (f32[2,144,128]{2,1,0:T(8,128)S(1)}, f32[144,128]{1,0:T(8,128)S(1)}, f32[144,128]{1,0:T(8,128)S(1)}, f32[2592,128]{1,0:T(8,128)S(1)}, f32[8,128]{1,0:T(8,128)S(1)}) custom-call(f32[2,144,128]{2,1,0:T(8,128)} %bitcast.12, f32[144,128]{1,0:T(8,128)} %bitcast.13, f32[144,128]{1,0:T(8,128)} %bitcast.14, f32[2592,128]{1,0:T(8,128)} %bitcast.11, ...), custom_call_target="tpu_custom_call" | custom-call | tf_op jit(solution)/shard_map/pallas_call | solution.py:826
  16.8 1.7 %shard_map.174 = (f32[2,144,128]{2,1,0:T(8,128)}, f32[144,128]{1,0:T(8,128)}, f32[144,128]{1,0:T(8,128)}, f32[2592,128]{1,0:T(8,128)}, f32[2]{0:T(128)}) custom-call(f32[2,144,128]{2,1,0:T(8,128)S(1)} %get-tuple-element.15.wind, f32[144,128]{1,0:T(8,128)S(1)} %get-tuple-element.16.temp, f32[144,128]{1,0:T(8,128)S(1)} %get-tuple-element.17.thick, ...), custom_call_target="tpu_custom_call" | custom-call | tf_op jit(solution)/shard_map/pallas_call | solution.py:878

commit v2 on v1

--- a/solution.py
+++ b/solution.py
@@ -69,10 +69,13 @@
 
 
 def packing(levels, chunks):
+    sizes = [(c[1] // 8, c[2] - (c[1] - 8)) for c in chunks]
+    sizes += [(2 * (levels // 8) + 1, 2 * (levels % 8))] * 2
     out = [(0, 1, 1)]
-    for tiles in [c[1] // 8 for c in chunks] + [2 * (levels // 8) + 1] * 2:
+    for tiles, left in sizes:
         quads = (tiles - 1) // 4
-        out.append((quads, tiles - quads, 8 * (tiles - quads)))
+        width = tiles - quads
+        out.append((quads, width, 8 * width - (4 if left <= 4 else 0)))
     return out
 
 
@@ -191,7 +194,8 @@
         nt - 1 + (nl - 1) * (1 + tile) + face + one(has_dn)
         + 2 * (one(has_up) + one(has_dn) + one(at_end))
     )
-    unknown = (nt - 1 - tile) * (nl - 1) + jnp.maximum(nf - 2 - face, 0) + 2 * one(face == 0)
+    unknown = jnp.maximum(nf - 2 - face, 0) + 2 * one(face == 0)
+    beside = (nt - 1 - tile) * (nl - 1)
 
     def enter():
         pl.semaphore_wait(barrier, known)
@@ -208,7 +212,12 @@
             for p in range(1, nl):
                 @pl.when(tile - o >= 0)
                 def _():
-                    notify(chain_sem.at[0], (face, tile - o, lax.rem(lev + p, nl)))
+                    notify(chain_sem.at[1], (face, tile - o, lax.rem(lev + p, nl)))
+
+    def plane_meets():
+        @pl.when(beside > 0)
+        def _():
+            pl.semaphore_wait(chain_sem.at[1], beside)
 
     def ends_meet():
         @pl.when(unknown > 0)
@@ -328,6 +337,12 @@
         out = [tile_at(start + half + 8 * i) for half in (0, pad) for i in range(full)]
         second = pltpu.roll(tile_at(start + pad + 8 * full), tail, 0)
         return out + [jnp.where(sublane < tail, tile_at(start + 8 * full), second)]
+
+    def end_spots(j, i, x):
+        spot = 3 * quarter + 1
+        if packed[j][2] % 8 == 0:
+            return [(spot + i, x)]
+        return [(spot + 2 * i, x), (spot + 2 * i + 1, pltpu.roll(x, 4, 0))]
 
     def squeeze_rows(j):
         quads = packed[j][0]
@@ -345,10 +360,10 @@
                     ))
             done += thin[4 * quads :]
             for i in range(4 * quads):
-                spot = 3 * quarter + 1 + i
-                done[-1] = jnp.where(
-                    lane == spot, pltpu.roll(wide[i], (spot + 1) % columns, 1), done[-1]
-                )
+                for spot, x in end_spots(j, i, wide[i]):
+                    done[-1] = jnp.where(
+                        lane == spot, pltpu.roll(x, (spot + 1) % columns, 1), done[-1]
+                    )
             for i, x in enumerate(done):
                 out[at + 8 * i : at + 8 * i + 8, :] = x
 
@@ -409,11 +424,30 @@
                 out = jnp.where(within < unit // 2, out, folded)
             corner[which, d] = out
 
+    def corner_copy(which, d):
+        part = pl.ds(0, 4 if which else 1)
+        send(corner.at[which, d, part], corner_in.at[which, d, part],
+             corner_sem.at[which], diagonals[d])
+
+    def corners_known(which):
+        corner_copy(which, 0)
+        corner_copy(which, 1)
+
+        @pl.when(has_up)
+        def _():
+            corner_copy(which, 2)
+            corner_copy(which, 3)
+
+    def corners_rest(which):
+        @pl.when(face == 0)
+        def _():
+            corner_copy(which, 2)
+            corner_copy(which, 3)
+        del sent[-2:]
+
     def ship_corners(which):
-        part = pl.ds(0, 4 if which else 1)
         for d in range(4):
-            send(corner.at[which, d, part], corner_in.at[which, d, part],
-                 corner_sem.at[which], diagonals[d])
+            corner_copy(which, d)
 
     east = [level_rows(wind.at[0], a) for a in range(rows)]
     north = [level_rows(wind.at[1], a) for a in range(rows)]
@@ -438,6 +472,14 @@
                 a_ref[a, k * levels : k * levels + n, :] = pair[0][:n]
                 b_ref[a, k * levels : k * levels + n, :] = pair[1][:n]
 
+    def gathered(stage, base, count):
+        best = peak[stage]
+        if count:
+            drain(2 * count, peak_sem.at[stage])
+        for o in range(count):
+            best = jnp.maximum(best, peak_in[base + o])
+        return best
+
     def put_mass():
         whole_rows = lanes_plain(jnp.concatenate(
             [jnp.broadcast_to(x, (8, columns)) for x in merged(mass)], 0
@@ -445,25 +487,32 @@
         for r in range(distinct):
             put(0, 0, r, whole_rows[8 * r : 8 * r + 8])
 
-    def tracers_of(k):
+    def tracers_of(k, wanted=tuple(range(distinct))):
         start, count, _ = chunks[k]
         q = [tracer[pl.ds(start * rows + a, count, stride=rows), :] for a in range(rows)]
         first = [q[a] * a_ref[a, :count, :] for a in range(rows)]
-        keep = [mass[a] * q[a] - along_rows(first, a, step_d[a]) for a in range(rows)]
-        second = [q[a] * b_ref[a, :count, :] for a in range(rows)]
-        for r, (x, y) in enumerate(zip(merged(keep), merged(second))):
-            put(pieces[k + 1][0], 0, r, lanes_both(x, y))
-
+        x, y = {}, {}
+        for a in range(rows):
+            r = rep[a]
+            if r in wanted:
+                keep = mass[a] * q[a] - along_rows(first, a, step_d[a])
+                second = q[a] * b_ref[a, :count, :]
+                x[r], y[r] = (x[r] + keep, y[r] + second) if r in x else (keep, second)
+        for r in wanted:
+            put(pieces[k + 1][0], 0, r, lanes_both(x[r], y[r]))
 
     def ready(j):
         squeeze_rows(j)
         return pack_sides(j)
 
     traced[0].wait()
-    tracers_of(0)
-    made = ready(1)
+    insides, borders = tuple(range(1, distinct - 1)), (0, distinct - 1)
+    tracers_of(0, borders)
+    squeeze_rows(1)
     enter()
     ship_near(1)
+    tracers_of(0, insides)
+    made = pack_sides(1)
     ship_sides(1)
 
     drain(group_rows[1], in_sem.at[1])
@@ -474,15 +523,15 @@
     mass_made = pack_sides(0)
     pack_corners(0, mass_made)
     made += ready(2)
+    ship_near(2)
     send_totals()
-    ship_near(2)
     ship_sides(2)
     ship_near(0)
     ship_sides(0)
+    corners_known(0)
 
     drain(group_rows[3], in_sem.at[3])
     traced[2].wait()
-    tracers_of(2)
     depth = [level_rows(thick, a) for a in range(rows)]
     depth_c = by_column(depth)
     flux_a, flux_b = [], []
@@ -500,6 +549,14 @@
     peak[0] = jnp.concatenate(
         [time_step * speed, (time_step * viscosity) * damp, jnp.zeros((6, columns), f32)], 0
     )
+    tracers_of(2)
+    made += ready(3)
+    plane_meets()
+    for o, peer in enumerate(plane):
+        send(peak.at[0, pl.ds(0, 2)], peak_in.at[o, pl.ds(0, 2)], peak_sem.at[0], peer)
+    ship_near(3)
+    ship_sides(3)
+
     first, second, keep = [], [], []
     for a in range(rows):
         aa = jac[a] * (m[0][a] * east[a] + m[1][a] * north[a])
@@ -519,30 +576,25 @@
         value.append(mass[a] * (warm[a] - time_step * (east[a] * gx + north[a] * gy)))
     for r, x in enumerate(merged(value)):
         put(pieces[heat][0], 0, r, lanes_plain(x))
-    made += ready(3)
     made += ready(heat)
-    ship_near(3)
-    ship_sides(3)
+    pack_corners(1, made)
+    corners_known(1)
     ship_near(heat)
     ship_sides(heat)
 
     traced[3].wait()
     tracers_of(3)
-    pack_corners(1, made)
     later = ready(4)
     ends_meet()
-    ship_corners(0)
-    for o, peer in enumerate(plane):
-        send(peak.at[0, pl.ds(0, 2)], peak_in.at[o, pl.ds(0, 2)], peak_sem.at[0], peer)
+    corners_rest(0)
     ship_near(4)
     ship_sides(4)
-    ship_corners(1)
+    corners_rest(1)
     for j in (0, 1, 2, 3, heat, 4):
         ship_wrap(j)
 
     if nl > 1:
         drain((nl - 1) * rows, total_sem.at[0])
-    traced[4].wait()
     above = ground[...]
     for o in range(nl - 1):
         origin = lax.rem(lev + nl - (o + 1), nl)
@@ -562,37 +614,18 @@
     for r, (x, y) in enumerate(zip(merged(value_u), merged(value_v))):
         put(pieces[last][0], 0, r, lanes_plain(x))
         put(pieces[last][0], pad, r, lanes_plain(y))
-    tracers_of(4)
     later += ready(last)
-    later += ready(5)
     pack_corners(2, later)
-    ship_sides(last)
-    ship_sides(5)
     ship_corners(2)
     ship_rows(last)
+    ship_sides(last)
+
+    traced[4].wait()
+    tracers_of(4)
+    pack_corners(3, ready(5))
+    ship_corners(3)
     ship_rows(5)
-
-    def spread_peaks():
-        best = peak[0]
-        if plane:
-            drain(2 * len(plane), peak_sem.at[0])
-        for o in range(len(plane)):
-            best = jnp.maximum(best, peak_in[o])
-        peak[1] = best
-        for o in range(1, nf):
-            send(peak.at[1, pl.ds(0, 2)], peak_in.at[len(plane) + o - 1, pl.ds(0, 2)],
-                 peak_sem.at[1], (lax.rem(face + o, nf), tile, lev))
-
-    spread_peaks()
-
-    def gathered(stage, base, count):
-        best = peak[stage]
-        if count:
-            drain(2 * count, peak_sem.at[stage])
-        for o in range(count):
-            best = jnp.maximum(best, peak_in[base + o])
-        return best
-
+    ship_sides(5)
     for load in tables:
         load.wait()
 
@@ -685,9 +718,12 @@
                           pltpu.roll(three, 3 * quarter, 1)),
             )
             for x in (one, two, three, four):
-                spot = 3 * quarter + 1 + len(out)
+                spots = [p for p, _ in end_spots(j, len(out), x)]
                 x = jnp.take_along_axis(x, inner[which], axis=1)
-                end = jnp.broadcast_to(ends[:, spot : spot + 1], (8, columns))
+                parts = [jnp.broadcast_to(ends[:, p : p + 1], (8, columns)) for p in spots]
+                end = parts[0]
+                if len(parts) > 1:
+                    end = jnp.where(sublane < 4, end, pltpu.roll(parts[1], 4, 0))
                 out.append(jnp.where(rim_end[which], end, x))
         for x in got[3 * quads :]:
             out.append(jnp.take_along_axis(x, spread[which], axis=1))
@@ -696,7 +732,7 @@
             out = out[:full] + out[-1:] + out[full : 2 * full] + [second]
         return out
 
-    sets = [[0], [1, 2, 3, heat], [4, last, last, 5]]
+    sets = [[0], [1, 2, 3, heat], [4, last, last], [5]]
     corner_spot = {j: (w, group.index(j)) for w, group in enumerate(sets) for j in group}
 
     def sides_of(j):
@@ -739,7 +775,6 @@
                 ref[pl.ds((begin + 8 * i) * rows + a, n, stride=rows), :] = (x * inverse[a])[:n]
 
     inverse = [None] * rows
-    insides, borders = range(1, distinct - 1), (0, distinct - 1)
 
     def finish(j, seams, which_rows, both=None):
         start, total_count, packs = pieces[j]
@@ -766,22 +801,32 @@
                     stored(ref, 0, k, levels, r, x)
 
     groups = pad // 8
-    order = [0, 1, 2, 3, heat, 4, last, 5]
-    for j in order:
-        drain(2 * side_rows[j], side_sem.at[j])
-    for j in order:
-        seams = sides_of(j)
-        for i, x in enumerate(seams):
-            seam_x[first_pack[j] + i] = x
-        finish(j, seams, insides)
-    for block in (sets[0] + sets[1], list(dict.fromkeys(sets[2]))):
-        for j in block:
+    def finish_insides(order):
+        for j in order:
+            drain(2 * side_rows[j], side_sem.at[j])
+        for j in order:
+            seams = sides_of(j)
+            for i, x in enumerate(seams):
+                seam_x[first_pack[j] + i] = x
+            finish(j, seams, insides)
+
+    def finish_borders(order, corners):
+        for j in order:
             drain(2 * packed[j][2], piece_sem.at[j])
-        if 0 in block:
-            drain(4, corner_sem.at[0])
-        drain(16, corner_sem.at[1 if 0 in block else 2])
-        for j in block:
+        for which in corners:
+            drain(16 if which else 4, corner_sem.at[which])
+        for j in order:
             finish(j, with_corners(j), borders, rims_of(j))
+
+    finish_insides([0, 1, 2, 3, heat, 4])
+    peak[1] = gathered(0, 0, len(plane))
+    for o in range(1, nf):
+        send(peak.at[1, pl.ds(0, 2)], peak_in.at[len(plane) + o - 1, pl.ds(0, 2)],
+             peak_sem.at[1], (lax.rem(face + o, nf), tile, lev))
+    finish_borders([0, 1, 2, 3, heat], [0, 1])
+    finish_insides([last, 5])
+    finish_borders([4, last], [2])
+    finish_borders([5], [3])
 
     bound_o[...] = gathered(1, len(plane), nf - 1)
     drain(sum(sent), sent_sem.at[0])
@@ -847,14 +892,14 @@
             pltpu.VMEM((landing, columns), f32),
             pltpu.VMEM((packs, 8, columns), f32),
             pltpu.VMEM((packs, 8, columns), f32),
-            pltpu.VMEM((3, 4, 8, columns), f32),
+            pltpu.VMEM((4, 4, 8, columns), f32),
             pltpu.VMEM((rows, columns), f32),
-            pltpu.VMEM((2, 8, columns), f32),
+            pltpu.VMEM((3, 8, columns), f32),
             pltpu.VMEM((landing, columns), f32),
             pltpu.VMEM((landing, columns), f32),
             pltpu.VMEM((packs, 8, columns), f32),
             pltpu.VMEM((packs, 8, columns), f32),
-            pltpu.VMEM((3, 4, 8, columns), f32),
+            pltpu.VMEM((4, 4, 8, columns), f32),
             pltpu.VMEM((nl - 1, rows, columns), f32),
             pltpu.VMEM((peers, 8, columns), f32),
             pltpu.SMEM((nf, 2, nt), jnp.int32),
@@ -864,10 +909,10 @@
             dma((1,)),
             dma((pieces,)),
             dma((pieces,)),
+            dma((4,)),
+            dma((1,)),
             dma((3,)),
-            dma((1,)),
-            dma((2,)),
-            pltpu.SemaphoreType.REGULAR((1,)),
+            pltpu.SemaphoreType.REGULAR((2,)),
         ],
         compiler_params=pltpu.CompilerParams(collective_id=0, has_side_effects=True),
     )(

time: 18.7 us -> 18.1 us (0.968)
  the two profiles are of different devices: /device:TPU:1 before, /device:TPU:0 now
where the time goes in v2:
time: 18.1 us; the launch traced here: 17.9 us
  Pallas kernels  17.3 us (96%)
  between operations  0.64 us (4%)
    pallas_call x1, Pallas kernels, on_device(): pl.pallas_call(functools.partial(kernel, sizes, (levels, rows, columns, c...  15.6 us
    pallas_call x1, Pallas kernels, on_device(): pl.pallas_call(write_out, out_shape=tuple((jax.ShapeDtypeStruct(x, f32) f...  1.7 us

profile of v2, /device:TPU:0, one launch (start us, length us, event | category | flops | bytes accessed | tf_op | source)
XLA Modules:
  0.0 17.9 jit_solution(14748825225320061455)
XLA Ops:
  0.6 15.6 %shard_map.173 = (f32[2,144,128]{2,1,0:T(8,128)S(1)}, f32[144,128]{1,0:T(8,128)S(1)}, f32[144,128]{1,0:T(8,128)S(1)}, f32[2592,128]{1,0:T(8,128)S(1)}, f32[8,128]{1,0:T(8,128)S(1)}) custom-call(f32[2,144,128]{2,1,0:T(8,128)} %bitcast.12, f32[144,128]{1,0:T(8,128)} %bitcast.13, f32[144,128]{1,0:T(8,128)} %bitcast.14, f32[2592,128]{1,0:T(8,128)} %bitcast.11, ...), custom_call_target="tpu_custom_call" | custom-call | tf_op jit(solution)/shard_map/pallas_call | solution.py:871
  16.2 1.7 %shard_map.174 = (f32[2,144,128]{2,1,0:T(8,128)}, f32[144,128]{1,0:T(8,128)}, f32[144,128]{1,0:T(8,128)}, f32[2592,128]{1,0:T(8,128)}, f32[2]{0:T(128)}) custom-call(f32[2,144,128]{2,1,0:T(8,128)S(1)} %get-tuple-element.15.wind, f32[144,128]{1,0:T(8,128)S(1)} %get-tuple-element.16.temp, f32[144,128]{1,0:T(8,128)S(1)} %get-tuple-element.17.thick, ...), custom_call_target="tpu_custom_call" | custom-call | tf_op jit(solution)/shard_map/pallas_call | solution.py:923

commit v3 on v2

--- a/solution.py
+++ b/solution.py
@@ -832,13 +832,15 @@
     drain(sum(sent), sent_sem.at[0])
 
 
-def write_out(wind, temp, thick, tracer, bound, wind_o, temp_o, thick_o, tracer_o, bound_o, sem):
+def write_out(wind, temp, thick, tracer, bound, wind_o, temp_o, thick_o, tracer_o, bound_o, pair, sem):
     pairs = ((tracer, tracer_o), (wind, wind_o), (temp, temp_o), (thick, thick_o))
     copies = [pltpu.make_async_copy(a, b, sem.at[i]) for i, (a, b) in enumerate(pairs)]
     for copy in copies:
         copy.start()
-    bound_o[0] = jnp.max(bound[0:1, :])
-    bound_o[1] = jnp.max(bound[1:2, :])
+    pair[0] = jnp.max(bound[0:1, :])
+    pair[1] = jnp.max(bound[1:2, :])
+    copies.append(pltpu.make_async_copy(pair, bound_o, sem.at[4]))
+    copies[-1].start()
     for copy in copies:
         copy.wait()
 
@@ -924,8 +926,8 @@
         write_out,
         out_shape=tuple(jax.ShapeDtypeStruct(x, f32) for x in shapes[:4] + ((2,),)),
         in_specs=[vmem] * 5,
-        out_specs=(hbm,) * 4 + (smem,),
-        scratch_shapes=[dma((4,))],
+        out_specs=(hbm,) * 5,
+        scratch_shapes=[pltpu.SMEM((2,), f32), dma((5,))],
     )(*[pltpu.with_memory_space_constraint(x, pltpu.VMEM) for x in outs])
     return (
         outs[0].reshape(wind.shape), outs[1].reshape(temp.shape), outs[2].reshape(thick.shape),

time: 18.1 us -> 17.6 us (0.972)
  Pallas kernels: 17.3 us -> 16.8 us
    pallas_call x1, Pallas kernels: 1.7 us -> 1.2 us  [on_device(): pl.pallas_call(write_out, out_shape=tuple((jax.ShapeDtypeStruct(x, f32) f...]
where the time goes in v3:
time: 17.6 us; the launch traced here: 17.4 us
  Pallas kernels  16.8 us (95%)
  between operations  0.64 us (4%)
    pallas_call x1, Pallas kernels, on_device(): pl.pallas_call(functools.partial(kernel, sizes, (levels, rows, columns, c...  15.6 us
    pallas_call x1, Pallas kernels, on_device(): pl.pallas_call(write_out, out_shape=tuple((jax.ShapeDtypeStruct(x, f32) f...  1.2 us

profile of v3, /device:TPU:0, one launch (start us, length us, event | category | flops | bytes accessed | tf_op | source)
XLA Modules:
  0.0 17.4 jit_solution(1109752453669893743)
XLA Ops:
  0.6 15.6 %shard_map.173 = (f32[2,144,128]{2,1,0:T(8,128)S(1)}, f32[144,128]{1,0:T(8,128)S(1)}, f32[144,128]{1,0:T(8,128)S(1)}, f32[2592,128]{1,0:T(8,128)S(1)}, f32[8,128]{1,0:T(8,128)S(1)}) custom-call(f32[2,144,128]{2,1,0:T(8,128)} %bitcast.12, f32[144,128]{1,0:T(8,128)} %bitcast.13, f32[144,128]{1,0:T(8,128)} %bitcast.14, f32[2592,128]{1,0:T(8,128)} %bitcast.11, ...), custom_call_target="tpu_custom_call" | custom-call | tf_op jit(solution)/shard_map/pallas_call | solution.py:873
  16.2 1.2 %shard_map.174 = (f32[2,144,128]{2,1,0:T(8,128)}, f32[144,128]{1,0:T(8,128)}, f32[144,128]{1,0:T(8,128)}, f32[2592,128]{1,0:T(8,128)}, f32[2]{0:T(128)}) custom-call(f32[2,144,128]{2,1,0:T(8,128)S(1)} %get-tuple-element.15.wind, f32[144,128]{1,0:T(8,128)S(1)} %get-tuple-element.16.temp, f32[144,128]{1,0:T(8,128)S(1)} %get-tuple-element.17.thick, ...), custom_call_target="tpu_custom_call" | custom-call | tf_op jit(solution)/shard_map/pallas_call | solution.py:925
